TPU v7x, 256 devices: a whole 4x4x8 slice. The times are simulated.
256 devices in a mesh: prow: 8 (over z), pcol: 32 (over y, x, core).
Axes of the slice: x: 4, y: 4, z: 8, core: 2. Of those that a mesh axis runs over, the one named last changes fastest.
Arguments:
- points: float32 [1, 32, 2, 1024], P(None, 'pcol'), may hold values from 0 to 1
- range_length: float32 [1], replicated, may hold values from 0.05 to 0.15
- smoothness: int32 [1], replicated, may hold values from 0 to 2
- sketch_bank: bfloat16 [32, 48, 1024], P('pcol'), may hold values from -6 to 6
- sketch_ids: int32 [4, 8, 1, 32], P(None, 'prow', None, 'pcol'), may hold values from 0 to 31
- tile_ranks: int32 [4, 8, 1, 32], P(None, 'prow', None, 'pcol'), may hold values from 16 to 48
Outputs:
- y_factors: float32 [4, 8, 1, 32, 48, 1024], P(None, 'prow', None, 'pcol')
- c_factors: float32 [4, 8, 1, 32, 48, 1024], P(None, 'prow', None, 'pcol')
- tile_error: float32 [4, 8, 1, 32], P(None, 'prow', None, 'pcol')
- rank_total: int32 [1], replicated
All inputs are finite; a program needn't handle non-finite values.
Results may differ from a plain program's by a relative error of at most 0.0098.
The roundings to bfloat16 on the way count: a program that leaves them out, or rounds other values in their place, can miss the bound.
Values may be sent and summed in bfloat16 or wider, within the bound.
A program may use at most 64 MiB of HBM per device.

v0:
```python
import jax
import jax.numpy as jnp
from jax import lax
from jax.sharding import Mesh
from jax.sharding import PartitionSpec as P

PCOL = ("pcol_0", "pcol_1", "pcol_2")
PROW_PCOL = ("prow", "pcol_0", "pcol_1", "pcol_2")


def joined_along(parts, dim):
    shape = list(parts.shape[1:])
    shape[dim] *= parts.shape[0]
    return jnp.moveaxis(parts, 0, dim).reshape(shape)


def sent_to_all(x, axis):
    copies = jnp.broadcast_to(x, (lax.axis_size(axis), *x.shape))
    return lax.all_to_all(copies, axis, split_axis=0, concat_axis=0, tiled=True)


def collect(x, axis, dim):
    return joined_along(sent_to_all(x, axis), dim)


def one_axis_at_a_time(x, axes):
    for axis in axes:
        x = lax.psum(x, axis)
    return x


def kernel_factors(smoothness, range_length):
    morton_value = smoothness[0].astype(jnp.float32)
    kernel_scale = jnp.sqrt(2.0 * morton_value + 1.0) / range_length[0]
    linear_factor = jnp.where(smoothness[0] >= 1, 1.0, 0.0).astype(jnp.float32)
    squared_distance = jnp.where(smoothness[0] >= 2, 1.0 / 3.0, 0.0).astype(jnp.float32)
    return (kernel_scale, linear_factor, squared_distance)


def covariance_tile(row_locations, column_locations, kernel_scale, linear_factor, squared_distance):
    offset_horizontal = row_locations[0][:, None] - column_locations[0][None, :]
    offset_vertical = row_locations[1][:, None] - column_locations[1][None, :]
    scaled_distance = kernel_scale * jnp.sqrt(
        offset_horizontal * offset_horizontal + offset_vertical * offset_vertical
    )
    return (
        1.0 + linear_factor * scaled_distance + squared_distance * scaled_distance * scaled_distance
    ) * jnp.exp(-scaled_distance)


def compress(tile_low, sketch, rank):
    keep = jnp.arange(sketch.shape[0]) < rank
    sketch = jnp.where(keep[:, None], sketch, jnp.zeros_like(sketch))
    sketched = lax.dot_general(
        sketch, tile_low, (((1,), (1,)), ((), ())), preferred_element_type=jnp.float32
    )
    product = jnp.dot(sketched.astype(jnp.bfloat16), tile_low, preferred_element_type=jnp.float32)
    gram = jnp.dot(sketched, sketched.T, precision=lax.Precision.HIGHEST)
    shift = 0.1 * jnp.trace(gram) / rank.astype(jnp.float32)
    gram = gram + jnp.diag(jnp.where(keep, shift, jnp.ones_like(shift)))
    factor = jnp.linalg.cholesky(gram)
    coeffs = jax.scipy.linalg.cho_solve((factor, True), product)
    approx = lax.dot_general(
        sketched, coeffs, (((0,), (0,)), ((), ())), precision=lax.Precision.HIGHEST
    )
    error = tile_low.astype(jnp.float32) - approx
    return (sketched, coeffs, jnp.sum(error * error))


def per_device(points, range_length, smoothness, sketch_bank, sketch_ids, tile_ranks):
    row_count = lax.axis_size("prow")
    col_count = lax.axis_size(PCOL)
    row_place = lax.axis_index("prow")
    col_place = lax.axis_index(PCOL)
    row_tiles = sketch_ids.shape[0]
    col_tiles = sketch_ids.shape[2]
    tile_size = points.shape[3]
    sketch_rows = sketch_bank.shape[1]
    slots_total = row_tiles * col_tiles
    tiles_across = col_tiles * col_count
    kernel_scale, linear_factor, squared_distance = kernel_factors(smoothness, range_length)
    gathered = collect(points, PCOL, 1)
    every_block = gathered.reshape(tiles_across, 2, tile_size)
    row_index = jnp.arange(row_tiles, dtype=jnp.int32) * row_count + row_place
    col_index = jnp.arange(col_tiles, dtype=jnp.int32) * col_count + col_place
    slot_row = jnp.repeat(row_index, col_tiles)
    slot_col = jnp.tile(col_index, row_tiles)
    own_ids = sketch_ids.reshape(slots_total)
    own_ranks = tile_ranks.reshape(slots_total)
    lower = slot_col <= slot_row
    offdiag = slot_col < slot_row
    ranks_local = jnp.sum(jnp.where(offdiag, own_ranks, 0))
    rank_sum = one_axis_at_a_time(ranks_local, PROW_PCOL)
    bank_whole = lax.all_gather(sketch_bank, PCOL, axis=0, tiled=True)
    chosen = bank_whole[own_ids]
    row_points_all = every_block[slot_row]
    col_points_all = every_block[slot_col]

    def one_tile(row_locations, column_locations, sketch, rank):
        tile_block = covariance_tile(
            row_locations, column_locations, kernel_scale, linear_factor, squared_distance
        )
        norm_sq = jnp.sum(tile_block * tile_block)
        sketched, coeffs, err_sq = compress(tile_block.astype(jnp.bfloat16), sketch, rank)
        return (sketched, coeffs, norm_sq, err_sq)

    def mapped(inputs):
        return one_tile(inputs[0], inputs[1], inputs[2], inputs[3])

    sketched_all, coeffs_all, norm_all, err_all = lax.map(
        mapped, (row_points_all, col_points_all, chosen, own_ranks)
    )
    norm_local = jnp.sum(jnp.where(lower, jnp.where(offdiag, 2.0, 1.0) * norm_all, 0.0))
    total = one_axis_at_a_time(norm_local, PROW_PCOL)
    errors = (
        jnp.where(offdiag, jnp.sqrt(err_all), jnp.sqrt(norm_all)) * tiles_across / jnp.sqrt(total)
    )
    errors = jnp.where(lower, errors, 0.0)
    out_shape = (row_tiles, 1, col_tiles, 1, sketch_rows, tile_size)
    y_out = jnp.where(offdiag[:, None, None], sketched_all, 0.0).reshape(out_shape)
    c_out = jnp.where(offdiag[:, None, None], coeffs_all, 0.0).reshape(out_shape)
    err_out = errors.reshape(row_tiles, 1, col_tiles, 1)
    rank_out = rank_sum.reshape(1)
    return (y_out, c_out, err_out, rank_out)


def solution(mesh):
    split = Mesh(
        mesh.devices.reshape(mesh.shape["prow"], 4, 4, 2), ("prow", "pcol_0", "pcol_1", "pcol_2")
    )
    placed = (
        P(None, PCOL, None, None),
        P(),
        P(),
        P(PCOL, None, None),
        P(None, "prow", None, PCOL),
        P(None, "prow", None, PCOL),
    )
    return jax.shard_map(
        per_device,
        mesh=split,
        in_specs=placed,
        out_specs=(
            P(None, "prow", None, PCOL, None, None),
            P(None, "prow", None, PCOL, None, None),
            P(None, "prow", None, PCOL),
            P(),
        ),
        check_vma=False,
    )
```

profile of v0, /device:TPU:1, one launch (start us, length us, event | category | flops | bytes accessed | tf_op | source)
XLA Modules:
  0.0 285.3 jit_solution(14311572031564186619)
XLA Ops:
  9.4 8.6 %all-to-all-start = ((f32[32,1,1,2,1024]{4,3,2,1,0:T(2,128)}), f32[32,1,1,2,1024]{4,3,2,1,0:T(2,128)S(1)}, u32[]{:S(2)}, u32[]{:S(2)}) async-start(f32[32,1,1,2,1024]{4,3,2,1,0:T(2,128)} %broadcast_in_dim.93), calls=%async_computation | async-start | bytes 524288 | tf_op jit(solution)/shard_map/all_to_all | solution.py:19
  21.4 5.4 %all-to-all-done = f32[32,1,1,2,1024]{4,3,2,1,0:T(2,128)S(1)} async-done(((f32[32,1,1,2,1024]{4,3,2,1,0:T(2,128)}), f32[32,1,1,2,1024]{4,3,2,1,0:T(2,128)S(1)}, u32[]{:S(2)}, u32[]{:S(2)}) %all-to-all-start) | async-done | bytes 262176 | tf_op jit(solution)/shard_map/all_to_all | solution.py:19
  28.0 36.6 %all-gather.2.cloned.1.call-done = bf16[32,48,1024]{2,1,0:T(8,128)(2,1)} async-done(((bf16[1,48,1024]{2,1,0:T(8,128)(2,1)}), bf16[32,48,1024]{2,1,0:T(8,128)(2,1)}) %all-gather.2.cloned.1.call-update) | async-done | bytes 3145744 | tf_op jit(solution)/shard_map/all_gather | solution.py:94
  67.2 136.1 %while.17 = (s32[]{:T(128)}, f32[4,48,1024]{2,1,0:T(8,128)S(1)}, f32[4,48,1024]{2,1,0:T(8,128)S(1)}, f32[4]{0:T(128)S(1)}, f32[4]{0:T(128)S(1)}, /*index=5*/s32[...) while((s32[]{:T(128)}, f32[4,48,1024]{2,1,0:T(8,128)S(1)}, ...), condition=%wide.region_6.7_spmd.clone, body=%wide.region_0.6_spmd.sunk.clone | while | flops 954344128 | bytes 2675283 | solution.py:110
  69.2 4.2 %multiply_reduce_fusion.6 = f32[]{:T(128)} fusion(f32[]{:T(128)} %get-tuple-element.278, f32[1024]{0:T(1024)S(1)} %bitcast.123, f32[1024]{0:T(1024)S(1)} %bitcast.127, f32[1024]{0:T(1024)S(1)} %bitcast.119, f32[1024]{0:T(1024)S(1)} %bitcast.131, f32[]{:T(128)} %get-tuple-element.275, f32[]{:T(128)} %get-tuple-element.274), kind=kLoop, calls=%fused_computation.7.clone.1.clone | loop fusion | flops 15728639 | bytes 16400 | tf_op jit(solution)/shard_map/while/body/eval_jaxpr/reduce_sum | solution.py:103
  79.9 4.4 %cholesky.73 = f32[48,48]{1,0:T(8,128)S(1)} custom-call(f32[48,48]{1,0:T(8,128)S(1)} %fusion.68), custom_call_target="Cholesky" | custom-call | tf_op jit(solution)/shard_map/while/body/eval_jaxpr/jit(cholesky)/cholesky | solution.py:61
  93.1 7.4 %multiply_reduce_fusion.7 = f32[]{:T(128)} fusion(f32[48,1024]{1,0:T(8,128)S(1)} %get-tuple-element.222, f32[48,1024]{1,0:T(8,128)S(1)} %get-tuple-element.226, f32[]{:T(128)} %get-tuple-element.278, f32[1024]{0:T(1024)S(1)} %bitcast.126, f32[1024]{0:T(1024)S(1)} %bitcast.130, f32[1024]{0:T(1024)S(1)} %bitcast.122, f32[1024]{0:T(1024)S(1)} %bitcast.134, ...), kind=kOutput, calls=%fused_computation.6.clone.1.clone | convolution fusion | flops 622854144 | bytes 409616 | tf_op jit(solution)/shard_map/while/body/eval_jaxpr/dot_general | solution.py:63
  103.2 4.2 %multiply_reduce_fusion.6 = f32[]{:T(128)} fusion(f32[]{:T(128)} %get-tuple-element.278, f32[1024]{0:T(1024)S(1)} %bitcast.123, f32[1024]{0:T(1024)S(1)} %bitcast.127, f32[1024]{0:T(1024)S(1)} %bitcast.119, f32[1024]{0:T(1024)S(1)} %bitcast.131, f32[]{:T(128)} %get-tuple-element.275, f32[]{:T(128)} %get-tuple-element.274), kind=kLoop, calls=%fused_computation.7.clone.1.clone | loop fusion | flops 15728639 | bytes 16400 | tf_op jit(solution)/shard_map/while/body/eval_jaxpr/reduce_sum | solution.py:103
  113.9 4.4 %cholesky.73 = f32[48,48]{1,0:T(8,128)S(1)} custom-call(f32[48,48]{1,0:T(8,128)S(1)} %fusion.68), custom_call_target="Cholesky" | custom-call | tf_op jit(solution)/shard_map/while/body/eval_jaxpr/jit(cholesky)/cholesky | solution.py:61
  127.2 7.4 %multiply_reduce_fusion.7 = f32[]{:T(128)} fusion(f32[48,1024]{1,0:T(8,128)S(1)} %get-tuple-element.222, f32[48,1024]{1,0:T(8,128)S(1)} %get-tuple-element.226, f32[]{:T(128)} %get-tuple-element.278, f32[1024]{0:T(1024)S(1)} %bitcast.126, f32[1024]{0:T(1024)S(1)} %bitcast.130, f32[1024]{0:T(1024)S(1)} %bitcast.122, f32[1024]{0:T(1024)S(1)} %bitcast.134, ...), kind=kOutput, calls=%fused_computation.6.clone.1.clone | convolution fusion | flops 622854144 | bytes 409616 | tf_op jit(solution)/shard_map/while/body/eval_jaxpr/dot_general | solution.py:63
  137.2 4.2 %multiply_reduce_fusion.6 = f32[]{:T(128)} fusion(f32[]{:T(128)} %get-tuple-element.278, f32[1024]{0:T(1024)S(1)} %bitcast.123, f32[1024]{0:T(1024)S(1)} %bitcast.127, f32[1024]{0:T(1024)S(1)} %bitcast.119, f32[1024]{0:T(1024)S(1)} %bitcast.131, f32[]{:T(128)} %get-tuple-element.275, f32[]{:T(128)} %get-tuple-element.274), kind=kLoop, calls=%fused_computation.7.clone.1.clone | loop fusion | flops 15728639 | bytes 16400 | tf_op jit(solution)/shard_map/while/body/eval_jaxpr/reduce_sum | solution.py:103
  147.9 4.4 %cholesky.73 = f32[48,48]{1,0:T(8,128)S(1)} custom-call(f32[48,48]{1,0:T(8,128)S(1)} %fusion.68), custom_call_target="Cholesky" | custom-call | tf_op jit(solution)/shard_map/while/body/eval_jaxpr/jit(cholesky)/cholesky | solution.py:61
  161.2 7.4 %multiply_reduce_fusion.7 = f32[]{:T(128)} fusion(f32[48,1024]{1,0:T(8,128)S(1)} %get-tuple-element.222, f32[48,1024]{1,0:T(8,128)S(1)} %get-tuple-element.226, f32[]{:T(128)} %get-tuple-element.278, f32[1024]{0:T(1024)S(1)} %bitcast.126, f32[1024]{0:T(1024)S(1)} %bitcast.130, f32[1024]{0:T(1024)S(1)} %bitcast.122, f32[1024]{0:T(1024)S(1)} %bitcast.134, ...), kind=kOutput, calls=%fused_computation.6.clone.1.clone | convolution fusion | flops 622854144 | bytes 409616 | tf_op jit(solution)/shard_map/while/body/eval_jaxpr/dot_general | solution.py:63
  171.2 4.2 %multiply_reduce_fusion.6 = f32[]{:T(128)} fusion(f32[]{:T(128)} %get-tuple-element.278, f32[1024]{0:T(1024)S(1)} %bitcast.123, f32[1024]{0:T(1024)S(1)} %bitcast.127, f32[1024]{0:T(1024)S(1)} %bitcast.119, f32[1024]{0:T(1024)S(1)} %bitcast.131, f32[]{:T(128)} %get-tuple-element.275, f32[]{:T(128)} %get-tuple-element.274), kind=kLoop, calls=%fused_computation.7.clone.1.clone | loop fusion | flops 15728639 | bytes 16400 | tf_op jit(solution)/shard_map/while/body/eval_jaxpr/reduce_sum | solution.py:103
  182.0 4.4 %cholesky.73 = f32[48,48]{1,0:T(8,128)S(1)} custom-call(f32[48,48]{1,0:T(8,128)S(1)} %fusion.68), custom_call_target="Cholesky" | custom-call | tf_op jit(solution)/shard_map/while/body/eval_jaxpr/jit(cholesky)/cholesky | solution.py:61
  187.7 3.7 %custom-call.20 = f32[1,48,48]{1,2,0:T(8,128)S(1)} custom-call(f32[1,48,48]{2,1,0:T(8,128)S(1)} %fusion.69), custom_call_target="InvertDiagBlocksLowerTriangular" | custom-call | tf_op jit(solution)/shard_map/while/body/eval_jaxpr/jit(_cho_solve)/triangular_solve | solution.py:62
  195.2 7.4 %multiply_reduce_fusion.7 = f32[]{:T(128)} fusion(f32[48,1024]{1,0:T(8,128)S(1)} %get-tuple-element.222, f32[48,1024]{1,0:T(8,128)S(1)} %get-tuple-element.226, f32[]{:T(128)} %get-tuple-element.278, f32[1024]{0:T(1024)S(1)} %bitcast.126, f32[1024]{0:T(1024)S(1)} %bitcast.130, f32[1024]{0:T(1024)S(1)} %bitcast.122, f32[1024]{0:T(1024)S(1)} %bitcast.134, ...), kind=kOutput, calls=%fused_computation.6.clone.1.clone | convolution fusion | flops 622854144 | bytes 409616 | tf_op jit(solution)/shard_map/while/body/eval_jaxpr/dot_general | solution.py:63
  204.0 11.7 %psum.60 = s32[]{:T(128)} all-reduce(s32[]{:T(128)} %select_reduce_fusion.2), channel_id=1, replica_groups=mesh['prow'=8,'pcol_0'=4,'pcol_1'=4,'pcol_2'=2] {'prow'}, use_global_device_ids=true, to_apply=%region_13.14 | all-reduce | flops 1 | bytes 8 | tf_op jit(solution)/shard_map/psum | solution.py:28
  215.6 11.8 %psum.56 = f32[]{:T(128)} all-reduce(f32[]{:T(128)} %fusion.22), channel_id=1, replica_groups=mesh['prow'=8,'pcol_0'=4,'pcol_1'=4,'pcol_2'=2] {'prow'}, use_global_device_ids=true, to_apply=%region_8.9 | all-reduce | flops 1 | bytes 8 | tf_op jit(solution)/shard_map/psum | solution.py:28
  227.4 6.9 %psum.61 = s32[]{:T(128)} all-reduce(s32[]{:T(128)} %psum.60), channel_id=1, replica_groups=mesh['prow'=8,'pcol_0'=4,'pcol_1'=4,'pcol_2'=2] {'pcol_0'}, use_global_device_ids=true, to_apply=%region_14.15 | all-reduce | flops 1 | bytes 8 | tf_op jit(solution)/shard_map/psum | solution.py:28
  234.3 8.1 %psum.57 = f32[]{:T(128)} all-reduce(f32[]{:T(128)} %psum.56), channel_id=1, replica_groups=mesh['prow'=8,'pcol_0'=4,'pcol_1'=4,'pcol_2'=2] {'pcol_0'}, use_global_device_ids=true, to_apply=%region_9.10 | all-reduce | flops 1 | bytes 8 | tf_op jit(solution)/shard_map/psum | solution.py:28
  242.4 6.2 %psum.62 = s32[]{:T(128)} all-reduce(s32[]{:T(128)} %psum.61), channel_id=1, replica_groups=mesh['prow'=8,'pcol_0'=4,'pcol_1'=4,'pcol_2'=2] {'pcol_1'}, use_global_device_ids=true, to_apply=%region_15.16 | all-reduce | flops 1 | bytes 8 | tf_op jit(solution)/shard_map/psum | solution.py:28
  248.6 7.7 %psum.58 = f32[]{:T(128)} all-reduce(f32[]{:T(128)} %psum.57), channel_id=1, replica_groups=mesh['prow'=8,'pcol_0'=4,'pcol_1'=4,'pcol_2'=2] {'pcol_1'}, use_global_device_ids=true, to_apply=%region_10.11 | all-reduce | flops 1 | bytes 8 | tf_op jit(solution)/shard_map/psum | solution.py:28
  256.3 16.5 %psum.63 = s32[1]{0:T(128)} all-reduce(s32[1]{0:T(128)} %bitcast.25), channel_id=1, replica_groups=mesh['prow'=8,'pcol_0'=4,'pcol_1'=4,'pcol_2'=2] {'pcol_2'}, use_global_device_ids=true, to_apply=%region_16.17 | all-reduce | flops 1 | bytes 8 | tf_op jit(solution)/shard_map/psum | solution.py:28
  (91 shorter events, 76.2 us)
Async XLA Ops:
  7.2 60.0 %copy-start = (s32[4,1,1,1]{0,3,2,1:T(1,128)S(1)}, s32[4,1,1,1]{0,3,2,1:T(1,128)}, u32[]{:S(2)}) copy-start(s32[4,1,1,1]{0,3,2,1:T(1,128)} %param.13) | copy-start | bytes 52
  7.2 57.4 %all-gather.2.cloned.1.call-start = ((), (), s32[]{:S(2)}) async-start(), calls=%async_computation.1 | async-start | bytes 3244032 | tf_op jit(solution)/shard_map/all_gather | solution.py:94
  9.4 17.5 %all-to-all-start = ((f32[32,1,1,2,1024]{4,3,2,1,0:T(2,128)}), f32[32,1,1,2,1024]{4,3,2,1,0:T(2,128)S(1)}, u32[]{:S(2)}, u32[]{:S(2)}) async-start(f32[32,1,1,2,1024]{4,3,2,1,0:T(2,128)} %broadcast_in_dim.93), calls=%async_computation | async-start | bytes 524288 | tf_op jit(solution)/shard_map/all_to_all | solution.py:19
Sparse Core Ops, SparseCore 0:
  10.5 53.9 all-gather.1
where the time goes:
time: 286 us; the launch traced here: 285 us
  blocking collectives  71.9 us (25%)
  other arithmetic  64.6 us (23%)
  matrix products  61.3 us (21%)
  waiting for transfers between devices  42.7 us (15%)
  between operations  16.2 us (6%)
  local copies, waits for them, and re-layouts  14.2 us (5%)
  starting transfers between devices  8.61 us (3%)
  loops' own time  5.85 us (2%)
    psum x8, blocking collectives, one_axis_at_a_time(): x = lax.psum(x, axis)  71.9 us
    all_gather x1, waiting for transfers between devices, per_device(): bank_whole = lax.all_gather(sketch_bank, PCOL, axis=0, tiled=True)  36.6 us
    dot_general x4, matrix products, compress(): lax.dot_general(sketched, coeffs, (((0,), (0,)), ((), ())), precision=lax...  29.4 us
    another operation x12, other arithmetic, compress(): factor = jnp.linalg.cholesky(gram)  20.2 us
    another operation x8, other arithmetic, compress(): coeffs = jax.scipy.linalg.cho_solve((factor, True), product)  17.3 us
    reduce_sum x4, other arithmetic, one_tile(): norm_sq = jnp.sum(tile_block * tile_block)  17 us
    dot_general x4, matrix products, compress(): jnp.dot(sketched.astype(jnp.bfloat16), tile_low, preferred_element_type=j...  12.7 us
    dot_general x4, matrix products, compress(): lax.dot_general(sketch, tile_low, (((1,), (1,)), ((), ())), preferred_ele...  12.6 us
  transfers between devices with their start and end apart: 2, of which 2 were waited for; matrix products, arithmetic and copies ran while one was open for 2% of the time, Pallas kernels for 0%

commit v1 on v0

--- a/solution.py
+++ b/solution.py
@@ -25,7 +25,7 @@
 
 def one_axis_at_a_time(x, axes):
     for axis in axes:
-        x = lax.psum(x, axis)
+        x = lax.all_gather(x, axis_name=axis).sum(axis=0)
     return x
 
 

time: 286 us -> 265 us (0.927)
  waiting for transfers between devices: 42.7 us -> 0.7 us
  local copies, waits for them, and re-layouts: 14.2 us -> 30.3 us
  other arithmetic: 64.6 us -> 69.5 us
    psum x8 -> x0, blocking collectives: 71.9 us -> none  [one_axis_at_a_time(): x = lax.psum(x, axis)]
    unnamed x0 -> x8, blocking collectives: none -> 69.3 us
    all_gather x1, waiting for transfers between devices: 36.6 us -> 0.02 us  [per_device(): bank_whole = lax.all_gather(sketch_bank, PCOL, axis=0, tiled=True)]
    unnamed x2 -> x20, local copies, waits for them, and re-layouts: 0.01 us -> 16.1 us
    all_to_all x1, waiting for transfers between devices: 5.43 us -> 0.01 us  [sent_to_all(): return lax.all_to_all(copies, axis, split_axis=0, concat_axis=0, tiled=True)]
    reduce_sum x0 -> x8, other arithmetic: none -> 5 us  [one_axis_at_a_time(): x = lax.all_gather(x, axis_name=axis).sum(axis=0)]
  transfers between devices with their start and end apart: 2 -> 2, of which waited for: 2 -> 0; matrix products, arithmetic and copies ran while one was open for 2% -> 7% of each run, Pallas kernels for 0% -> 0%
where the time goes in v1:
time: 265 us; the launch traced here: 264 us
  other arithmetic  69.5 us (26%)
  blocking collectives  69.3 us (26%)
  matrix products  61.3 us (23%)
  local copies, waits for them, and re-layouts  30.3 us (11%)
  between operations  16.2 us (6%)
  starting transfers between devices  10.7 us (4%)
  loops' own time  6.04 us (2%)
    unnamed x8, blocking collectives  69.3 us
    dot_general x4, matrix products, compress(): lax.dot_general(sketched, coeffs, (((0,), (0,)), ((), ())), precision=lax...  29.4 us
    another operation x12, other arithmetic, compress(): factor = jnp.linalg.cholesky(gram)  20.2 us
    another operation x8, other arithmetic, compress(): coeffs = jax.scipy.linalg.cho_solve((factor, True), product)  17.3 us
    reduce_sum x4, other arithmetic, one_tile(): norm_sq = jnp.sum(tile_block * tile_block)  17 us
    unnamed x20, local copies, waits for them, and re-layouts  16.1 us
    dot_general x4, matrix products, compress(): jnp.dot(sketched.astype(jnp.bfloat16), tile_low, preferred_element_type=j...  12.7 us
    dot_general x4, matrix products, compress(): lax.dot_general(sketch, tile_low, (((1,), (1,)), ((), ())), preferred_ele...  12.6 us
  transfers between devices with their start and end apart: 2, of which 0 were waited for; matrix products, arithmetic and copies ran while one was open for 7% of the time, Pallas kernels for 0%

profile of v1, /device:TPU:1, one launch (start us, length us, event | category | flops | bytes accessed | tf_op | source)
XLA Modules:
  0.0 264.0 jit_solution(12656178016808818181)
XLA Ops:
  11.8 14.0 %all-reduce.4 = s32[8]{0:T(128)S(1)} all-reduce(s32[8]{0:T(128)S(1)} %dynamic-update-slice.7), channel_id=1, replica_groups=mesh['prow'=8,'pcol_0'=4,'pcol_1'=4,'pcol_2'=2] {'prow'}, use_global_device_ids=true, to_apply=%add.4 | all-reduce | flops 8 | bytes 64
  30.5 10.6 %all-to-all-start = ((f32[32,1,1,2,1024]{4,3,2,1,0:T(2,128)}), f32[32,1,1,2,1024]{4,3,2,1,0:T(2,128)S(1)}, u32[]{:S(2)}, u32[]{:S(2)}) async-start(f32[32,1,1,2,1024]{4,3,2,1,0:T(2,128)} %broadcast_in_dim.93), calls=%async_computation | async-start | bytes 524288 | tf_op jit(solution)/shard_map/all_to_all | solution.py:19
  41.2 7.6 %all-reduce.5 = s32[4]{0:T(128)S(1)} all-reduce(s32[4]{0:T(128)S(1)} %dynamic-update-slice.8), channel_id=1, replica_groups=mesh['prow'=8,'pcol_0'=4,'pcol_1'=4,'pcol_2'=2] {'pcol_0'}, use_global_device_ids=true, to_apply=%add.5 | all-reduce | flops 4 | bytes 32
  52.9 7.3 %all-reduce.6 = s32[4]{0:T(128)S(1)} all-reduce(s32[4]{0:T(128)S(1)} %dynamic-update-slice.9), channel_id=1, replica_groups=mesh['prow'=8,'pcol_0'=4,'pcol_1'=4,'pcol_2'=2] {'pcol_1'}, use_global_device_ids=true, to_apply=%add.6 | all-reduce | flops 4 | bytes 32
  68.8 136.3 %while.16 = (s32[]{:T(128)}, f32[4,48,1024]{2,1,0:T(8,128)S(1)}, f32[4,48,1024]{2,1,0:T(8,128)S(1)}, f32[4]{0:T(128)S(1)}, f32[4]{0:T(128)S(1)}, /*index=5*/s32[...) while((s32[]{:T(128)}, f32[4,48,1024]{2,1,0:T(8,128)S(1)}, ...), condition=%wide.region_6.7_spmd, body=%wide.region_0.6_spmd.sunk | while | flops 954344128 | bytes 2675315 | solution.py:110
  71.0 4.2 %multiply_reduce_fusion.4 = f32[]{:T(128)} fusion(f32[]{:T(128)} %get-tuple-element.247, f32[1024]{0:T(1024)S(1)} %bitcast.115, f32[1024]{0:T(1024)S(1)} %bitcast.119, f32[1024]{0:T(1024)S(1)} %bitcast.111, f32[1024]{0:T(1024)S(1)} %bitcast.123, f32[]{:T(128)} %get-tuple-element.244, f32[]{:T(128)} %get-tuple-element.243), kind=kLoop, calls=%fused_computation.7.clone.1 | loop fusion | flops 15728639 | bytes 16400 | tf_op jit(solution)/shard_map/while/body/eval_jaxpr/reduce_sum | solution.py:103
  81.7 4.4 %cholesky.62 = f32[48,48]{1,0:T(8,128)S(1)} custom-call(f32[48,48]{1,0:T(8,128)S(1)} %fusion.55), custom_call_target="Cholesky" | custom-call | tf_op jit(solution)/shard_map/while/body/eval_jaxpr/jit(cholesky)/cholesky | solution.py:61
  87.4 3.7 %custom-call.17 = f32[1,48,48]{1,2,0:T(8,128)S(1)} custom-call(f32[1,48,48]{2,1,0:T(8,128)S(1)} %fusion.56), custom_call_target="InvertDiagBlocksLowerTriangular" | custom-call | tf_op jit(solution)/shard_map/while/body/eval_jaxpr/jit(_cho_solve)/triangular_solve | solution.py:62
  94.9 7.4 %multiply_reduce_fusion.5 = f32[]{:T(128)} fusion(f32[48,1024]{1,0:T(8,128)S(1)} %get-tuple-element.199, f32[48,1024]{1,0:T(8,128)S(1)} %get-tuple-element.203, f32[]{:T(128)} %get-tuple-element.247, f32[1024]{0:T(1024)S(1)} %bitcast.118, f32[1024]{0:T(1024)S(1)} %bitcast.122, f32[1024]{0:T(1024)S(1)} %bitcast.114, f32[1024]{0:T(1024)S(1)} %bitcast.126, ...), kind=kOutput, calls=%fused_computation.6.clone.1 | convolution fusion | flops 622854144 | bytes 409616 | tf_op jit(solution)/shard_map/while/body/eval_jaxpr/dot_general | solution.py:63
  105.0 4.2 %multiply_reduce_fusion.4 = f32[]{:T(128)} fusion(f32[]{:T(128)} %get-tuple-element.247, f32[1024]{0:T(1024)S(1)} %bitcast.115, f32[1024]{0:T(1024)S(1)} %bitcast.119, f32[1024]{0:T(1024)S(1)} %bitcast.111, f32[1024]{0:T(1024)S(1)} %bitcast.123, f32[]{:T(128)} %get-tuple-element.244, f32[]{:T(128)} %get-tuple-element.243), kind=kLoop, calls=%fused_computation.7.clone.1 | loop fusion | flops 15728639 | bytes 16400 | tf_op jit(solution)/shard_map/while/body/eval_jaxpr/reduce_sum | solution.py:103
  115.7 4.4 %cholesky.62 = f32[48,48]{1,0:T(8,128)S(1)} custom-call(f32[48,48]{1,0:T(8,128)S(1)} %fusion.55), custom_call_target="Cholesky" | custom-call | tf_op jit(solution)/shard_map/while/body/eval_jaxpr/jit(cholesky)/cholesky | solution.py:61
  121.4 3.7 %custom-call.17 = f32[1,48,48]{1,2,0:T(8,128)S(1)} custom-call(f32[1,48,48]{2,1,0:T(8,128)S(1)} %fusion.56), custom_call_target="InvertDiagBlocksLowerTriangular" | custom-call | tf_op jit(solution)/shard_map/while/body/eval_jaxpr/jit(_cho_solve)/triangular_solve | solution.py:62
  129.0 7.4 %multiply_reduce_fusion.5 = f32[]{:T(128)} fusion(f32[48,1024]{1,0:T(8,128)S(1)} %get-tuple-element.199, f32[48,1024]{1,0:T(8,128)S(1)} %get-tuple-element.203, f32[]{:T(128)} %get-tuple-element.247, f32[1024]{0:T(1024)S(1)} %bitcast.118, f32[1024]{0:T(1024)S(1)} %bitcast.122, f32[1024]{0:T(1024)S(1)} %bitcast.114, f32[1024]{0:T(1024)S(1)} %bitcast.126, ...), kind=kOutput, calls=%fused_computation.6.clone.1 | convolution fusion | flops 622854144 | bytes 409616 | tf_op jit(solution)/shard_map/while/body/eval_jaxpr/dot_general | solution.py:63
  139.0 4.2 %multiply_reduce_fusion.4 = f32[]{:T(128)} fusion(f32[]{:T(128)} %get-tuple-element.247, f32[1024]{0:T(1024)S(1)} %bitcast.115, f32[1024]{0:T(1024)S(1)} %bitcast.119, f32[1024]{0:T(1024)S(1)} %bitcast.111, f32[1024]{0:T(1024)S(1)} %bitcast.123, f32[]{:T(128)} %get-tuple-element.244, f32[]{:T(128)} %get-tuple-element.243), kind=kLoop, calls=%fused_computation.7.clone.1 | loop fusion | flops 15728639 | bytes 16400 | tf_op jit(solution)/shard_map/while/body/eval_jaxpr/reduce_sum | solution.py:103
  149.7 4.4 %cholesky.62 = f32[48,48]{1,0:T(8,128)S(1)} custom-call(f32[48,48]{1,0:T(8,128)S(1)} %fusion.55), custom_call_target="Cholesky" | custom-call | tf_op jit(solution)/shard_map/while/body/eval_jaxpr/jit(cholesky)/cholesky | solution.py:61
  163.0 7.4 %multiply_reduce_fusion.5 = f32[]{:T(128)} fusion(f32[48,1024]{1,0:T(8,128)S(1)} %get-tuple-element.199, f32[48,1024]{1,0:T(8,128)S(1)} %get-tuple-element.203, f32[]{:T(128)} %get-tuple-element.247, f32[1024]{0:T(1024)S(1)} %bitcast.118, f32[1024]{0:T(1024)S(1)} %bitcast.122, f32[1024]{0:T(1024)S(1)} %bitcast.114, f32[1024]{0:T(1024)S(1)} %bitcast.126, ...), kind=kOutput, calls=%fused_computation.6.clone.1 | convolution fusion | flops 622854144 | bytes 409616 | tf_op jit(solution)/shard_map/while/body/eval_jaxpr/dot_general | solution.py:63
  173.0 4.2 %multiply_reduce_fusion.4 = f32[]{:T(128)} fusion(f32[]{:T(128)} %get-tuple-element.247, f32[1024]{0:T(1024)S(1)} %bitcast.115, f32[1024]{0:T(1024)S(1)} %bitcast.119, f32[1024]{0:T(1024)S(1)} %bitcast.111, f32[1024]{0:T(1024)S(1)} %bitcast.123, f32[]{:T(128)} %get-tuple-element.244, f32[]{:T(128)} %get-tuple-element.243), kind=kLoop, calls=%fused_computation.7.clone.1 | loop fusion | flops 15728639 | bytes 16400 | tf_op jit(solution)/shard_map/while/body/eval_jaxpr/reduce_sum | solution.py:103
  183.8 4.4 %cholesky.62 = f32[48,48]{1,0:T(8,128)S(1)} custom-call(f32[48,48]{1,0:T(8,128)S(1)} %fusion.55), custom_call_target="Cholesky" | custom-call | tf_op jit(solution)/shard_map/while/body/eval_jaxpr/jit(cholesky)/cholesky | solution.py:61
  197.0 7.4 %multiply_reduce_fusion.5 = f32[]{:T(128)} fusion(f32[48,1024]{1,0:T(8,128)S(1)} %get-tuple-element.199, f32[48,1024]{1,0:T(8,128)S(1)} %get-tuple-element.203, f32[]{:T(128)} %get-tuple-element.247, f32[1024]{0:T(1024)S(1)} %bitcast.118, f32[1024]{0:T(1024)S(1)} %bitcast.122, f32[1024]{0:T(1024)S(1)} %bitcast.114, f32[1024]{0:T(1024)S(1)} %bitcast.126, ...), kind=kOutput, calls=%fused_computation.6.clone.1 | convolution fusion | flops 622854144 | bytes 409616 | tf_op jit(solution)/shard_map/while/body/eval_jaxpr/dot_general | solution.py:63
  207.1 5.1 %all-reduce.7 = s32[2]{0:T(128)S(1)} all-reduce(s32[2]{0:T(128)S(1)} %dynamic-update-slice.10), channel_id=1, replica_groups=mesh['prow'=8,'pcol_0'=4,'pcol_1'=4,'pcol_2'=2] {'pcol_2'}, use_global_device_ids=true, to_apply=%add.7 | all-reduce | flops 2 | bytes 16
  212.2 11.6 %all-reduce = f32[8]{0:T(128)S(1)} all-reduce(f32[8]{0:T(128)S(1)} %dynamic-update-slice.3), channel_id=1, replica_groups=mesh['prow'=8,'pcol_0'=4,'pcol_1'=4,'pcol_2'=2] {'prow'}, use_global_device_ids=true, to_apply=%add | all-reduce | flops 8 | bytes 64
  225.8 6.6 %all-reduce.1 = f32[4]{0:T(128)S(1)} all-reduce(f32[4]{0:T(128)S(1)} %dynamic-update-slice.4), channel_id=1, replica_groups=mesh['prow'=8,'pcol_0'=4,'pcol_1'=4,'pcol_2'=2] {'pcol_0'}, use_global_device_ids=true, to_apply=%add.1 | all-reduce | flops 4 | bytes 32
  234.4 6.9 %all-reduce.2 = f32[4]{0:T(128)S(1)} all-reduce(f32[4]{0:T(128)S(1)} %dynamic-update-slice.5), channel_id=1, replica_groups=mesh['prow'=8,'pcol_0'=4,'pcol_1'=4,'pcol_2'=2] {'pcol_1'}, use_global_device_ids=true, to_apply=%add.2 | all-reduce | flops 4 | bytes 32
  243.9 10.1 %all-reduce.3 = f32[2]{0:T(128)S(1)} all-reduce(f32[2]{0:T(128)S(1)} %dynamic-update-slice.6), channel_id=1, replica_groups=mesh['prow'=8,'pcol_0'=4,'pcol_1'=4,'pcol_2'=2] {'pcol_2'}, use_global_device_ids=true, to_apply=%add.3 | all-reduce | flops 2 | bytes 16
  (119 shorter events, 90.5 us)
Async XLA Ops:
  7.2 61.7 %copy-start = (s32[4,1,1,1]{0,3,2,1:T(1,128)S(1)}, s32[4,1,1,1]{0,3,2,1:T(1,128)}, u32[]{:S(2)}) copy-start(s32[4,1,1,1]{0,3,2,1:T(1,128)} %param.13) | copy-start | bytes 52
  7.2 59.0 %all-gather.2.cloned.1.call-start = ((), (), s32[]{:S(2)}) async-start(), calls=%async_computation.1 | async-start | bytes 3244032 | tf_op jit(solution)/shard_map/all_gather | solution.py:94
  30.5 34.4 %all-to-all-start = ((f32[32,1,1,2,1024]{4,3,2,1,0:T(2,128)}), f32[32,1,1,2,1024]{4,3,2,1,0:T(2,128)S(1)}, u32[]{:S(2)}, u32[]{:S(2)}) async-start(f32[32,1,1,2,1024]{4,3,2,1,0:T(2,128)} %broadcast_in_dim.93), calls=%async_computation | async-start | bytes 524288 | tf_op jit(solution)/shard_map/all_to_all | solution.py:19
Sparse Core Ops, SparseCore 0:
  10.5 54.0 all-gather.1
